TPU v7x, 32 devices: a whole 2x2x4 slice. The times are simulated.
32 devices in a mesh: section: 4 (over y, x), seq: 8 (over z, core).
Axes of the slice: x: 2, y: 2, z: 4, core: 2. Of those that a mesh axis runs over, the one named last changes fastest.
Arguments:
- patches: bfloat16 [8, 729, 1152], P('seq'), may hold values from -40 to 40
- fc_gain: float32 [4, 1152], P('section'), may hold values from 0.1 to 1.9
- fc_in: bfloat16 [4, 1152, 2176], P('section', 'seq'), may hold values from -0.1875 to 0.1875
- fc_in_bias: float32 [4, 2176], P('section'), may hold values from -3 to 3
- fc_out: bfloat16 [4, 2176, 1152], P('section', None, 'seq'), may hold values from -0.125 to 0.125
- fc_out_bias: float32 [4, 1152], P('section'), may hold values from -3 to 3
- proj_weight: bfloat16 [1152, 3584], P('seq'), may hold values from -0.1875 to 0.1875
- text_embed: bfloat16 [1024, 3584], P('seq'), may hold values from -40 to 40
- frame_start: int32 [8], replicated, may hold values from 0 to 1023, as said below
- frame_count: int32 [8], replicated, may hold values from 1 to 196, as said below
- segment_ids: int32 [1024], replicated, may hold values from 0 to 2, as said below
- norm_gain: float32 [3584], replicated, may hold values from 0.1 to 1.9
- query_weight: bfloat16 [3584, 2048], P(None, 'section'), may hold values from -3 to 3
- query_bias: float32 [2048], P('section'), may hold values from -3 to 3
- key_weight: bfloat16 [3584, 512], P(None, 'section'), may hold values from -1 to 1
- value_weight: bfloat16 [3584, 512], P(None, 'section'), may hold values from -0.09375 to 0.09375
- value_bias: float32 [512], P('section'), may hold values from -3 to 3
Outputs:
- attended: bfloat16 [1024, 2048], P('seq', 'section')
Inputs may be any that keep to these rules, and one draw needn't show every extreme that they name: Frame f keeps its first frame_count[f] pooled tokens and places them at positions frame_start[f] to frame_start[f] + frame_count[f] - 1; frame f begins in shard f, at a position from f * 128 to (f + 1) * 128 - 1; every frame ends before the next one begins, and the last ends by position 1023. The frame of shard 8 / 2 - 1 runs into the next shard. `frame_count`: some frame keeps all 196 tokens. `segment_ids`: segment numbers never fall along the sequence, and each of 0, 1 and 2 occurs.
All inputs are finite; a program needn't handle non-finite values.
Results may differ from a plain program's by a relative error of at most 0.02.
Values may be sent and summed in bfloat16 or wider, within the bound.
A program may use at most 128 MiB of HBM per device.

v0:
```python
import functools
import math

import jax
import jax.numpy as jnp
from jax import lax
from jax.experimental import pallas as pl
from jax.experimental.pallas import tpu as pltpu
from jax.sharding import PartitionSpec as P

GRID = 27


layer_eps = 1e-06
rms_eps = 1e-06
rope_base = 1000000.0
mask_floor = -1e30


def passed_along(block, axis, distance):
    devices = range(lax.axis_size(axis))
    route = [(i - distance, i) for i in devices if i - distance in devices]
    return lax.ppermute(block, axis, route)


def from_last(x, axis):
    last = lax.axis_size(axis) - 1
    total = x
    for other in range(last):
        total = total + lax.ppermute(x, axis, [(last, other)])
    return total


def layer_norm(values, scales):
    widened = values.astype(jnp.float32)
    center = widened - jnp.mean(widened, axis=-1, keepdims=True)
    spread = jnp.mean(center * center, axis=-1, keepdims=True)
    return center * lax.rsqrt(spread + layer_eps) * scales


def encoder_layer(values, scales, w_in, b_in, w_out, b_out):
    normed = layer_norm(values, scales).astype(jnp.bfloat16)
    hidden = jax.nn.gelu(
        jnp.dot(normed, w_in, preferred_element_type=jnp.float32) + b_in, approximate=True
    ).astype(jnp.bfloat16)
    summed = (
        values.astype(jnp.float32)
        + jnp.dot(hidden, w_out, preferred_element_type=jnp.float32)
        + b_out
    )
    return summed.astype(jnp.bfloat16)


MESH = pl.DeviceIdType.MESH


def greet(axis, targets):
    barrier = pltpu.get_barrier_semaphore()
    for target, present in targets:

        @pl.when(present)
        def _(target=target):
            pl.semaphore_signal(barrier, inc=1, device_id={axis: target}, device_id_type=MESH)

    peers = 0
    for _, present in targets:
        peers = peers + present.astype(jnp.int32)
    pl.semaphore_wait(barrier, peers)


def chain_kernel(count, *refs):
    srcs, outs = refs[:count], refs[count : 2 * count]
    up_s, up_r, dn_s, dn_r, pu_s, pu_r, pd_s, pd_r, own = refs[2 * count :]
    size = lax.axis_size("seq")
    chips = size // 2
    me = lax.axis_index("seq")
    chip, core = me // 2, me % 2
    partner = chip * 2 + 1 - core
    above = jnp.minimum(chip + 1, chips - 1) * 2 + core
    below = jnp.maximum(chip - 1, 0) * 2 + core
    has_up, has_down = chip < chips - 1, chip > 0

    def slot(m, j, c):
        rows = srcs[m].shape[0]
        return outs[m].at[pl.ds(pl.multiple_of((2 * j + c) * rows, rows), rows)]

    def copy(m, t, j, c, sems, target):
        return pltpu.make_async_remote_copy(
            src_ref=srcs[m] if t == 0 else slot(m, j, c),
            dst_ref=slot(m, j, c),
            send_sem=sems[0].at[t, m],
            recv_sem=sems[1].at[t, m],
            device_id={"seq": target},
            device_id_type=MESH,
        )

    up, down, pu, pd = (up_s, up_r), (dn_s, dn_r), (pu_s, pu_r), (pd_s, pd_r)
    greet("seq", [(above, has_up), (below, has_down), (partner, me >= 0)])
    for m in range(count):
        pltpu.make_async_copy(srcs[m], slot(m, chip, core), own.at[m]).start()
    for t in range(chips):
        for m in range(count):

            @pl.when(chip - t >= 0)
            def _(t=t, m=m):
                j = chip - t
                if t > 0:
                    copy(m, t - 1, j, core, up, above).wait_recv()

                @pl.when(has_up)
                def _():
                    copy(m, t, j, core, up, above).start()

                copy(m, t, j, core, pu, partner).start()

            @pl.when(chip + t < chips)
            def _(t=t, m=m):
                j = chip + t
                if t > 0:
                    copy(m, t - 1, j, core, down, below).wait_recv()

                @pl.when(has_down)
                def _():
                    copy(m, t, j, core, down, below).start()

                if t > 0:
                    copy(m, t, j, core, pd, partner).start()

    for m in range(count):
        pltpu.make_async_copy(srcs[m], slot(m, chip, core), own.at[m]).wait()
    for t in range(chips):
        for m in range(count):

            @pl.when(chip - t >= 0)
            def _(t=t, m=m):
                j = chip - t

                @pl.when(has_up)
                def _():
                    copy(m, t, j, core, up, above).wait_send()

                copy(m, t, j, core, pu, partner).wait_send()
                copy(m, t, j, 1 - core, pu, partner).wait_recv()

            @pl.when(chip + t < chips)
            def _(t=t, m=m):
                j = chip + t

                @pl.when(has_down)
                def _():
                    copy(m, t, j, core, down, below).wait_send()

                if t > 0:
                    copy(m, t, j, core, pd, partner).wait_send()
                    copy(m, t, j, 1 - core, pd, partner).wait_recv()


def chain_gather(blocks, call_id, where):
    size = lax.axis_size("seq")
    count = len(blocks)
    return pl.pallas_call(
        functools.partial(chain_kernel, count),
        out_shape=[
            jax.ShapeDtypeStruct((b.shape[0] * size, b.shape[1]), b.dtype) for b in blocks
        ],
        in_specs=[pl.BlockSpec(memory_space=pltpu.VMEM)] * count,
        out_specs=[pl.BlockSpec(memory_space=where)] * count,
        scratch_shapes=[pltpu.SemaphoreType.DMA((size // 2, count))] * 8
        + [pltpu.SemaphoreType.DMA((count,))],
        compiler_params=pltpu.CompilerParams(collective_id=call_id, has_side_effects=True),
    )(*blocks)


def encode_kernel(
    rows, patches, gain, w_in, b_in, w_out_t, b_out, out, inbox, send_sem, recv_sem
):
    section = lax.axis_index("section")
    sections = lax.axis_size("section")
    following = jnp.minimum(section + 1, sections - 1)
    batches = patches.shape[0] // rows
    first = section == 0
    not_first, not_last = section > 0, section < sections - 1
    greet("section", [(following, not_last), (jnp.maximum(section - 1, 0), not_first)])

    def copy(b):
        block = pl.ds(pl.multiple_of(b * rows, rows), rows)
        return pltpu.make_async_remote_copy(
            src_ref=out.at[block],
            dst_ref=inbox.at[block],
            send_sem=send_sem.at[b],
            recv_sem=recv_sem.at[b],
            device_id={"section": following},
            device_id_type=MESH,
        )

    def run(b, carry):
        block = pl.ds(pl.multiple_of(b * rows, rows), rows)

        @pl.when(first)
        def _():
            inbox[block, :] = patches[block, :]

        @pl.when(not_first)
        def _():
            copy(b).wait_recv()

        values = inbox[block, :]
        normed = layer_norm(values, gain[...]).astype(jnp.bfloat16)
        pre = jnp.dot(normed, w_in[...], preferred_element_type=jnp.float32) + b_in[...]
        hidden = jax.nn.gelu(pre, approximate=True).astype(jnp.bfloat16)
        mixed = lax.dot_general(
            hidden, w_out_t[...], (((1,), (1,)), ((), ())), preferred_element_type=jnp.float32
        )
        out[block, :] = (values.astype(jnp.float32) + mixed + b_out[...]).astype(jnp.bfloat16)

        @pl.when(not_last)
        def _():
            copy(b).start()

        return carry

    lax.fori_loop(0, batches, run, 0)

    @pl.when(not_last)
    def _():
        def drain(b, carry):
            copy(b).wait_send()
            return carry

        lax.fori_loop(0, batches, drain, 0)


def encode(patches, gain, w_in, b_in, w_out_t, b_out, rows, call_id):
    batches = patches.shape[0] // rows
    whole = pl.BlockSpec(memory_space=pltpu.VMEM)
    return pl.pallas_call(
        functools.partial(encode_kernel, rows),
        out_shape=jax.ShapeDtypeStruct(patches.shape, patches.dtype),
        in_specs=[whole] * 6,
        out_specs=whole,
        scratch_shapes=[
            pltpu.VMEM(patches.shape, patches.dtype),
            pltpu.SemaphoreType.DMA((batches,)),
            pltpu.SemaphoreType.DMA((batches,)),
        ],
        compiler_params=pltpu.CompilerParams(
            collective_id=call_id, has_side_effects=True, vmem_limit_bytes=48 * 1024 * 1024
        ),
    )(patches, gain[None], w_in, b_in[None], w_out_t, b_out[None])


def pool_rows(offsets, counts_kept, patch_rows):
    pool_side = (GRID + 1) // 2
    token_i = (offsets // pool_side)[:, None]
    token_j = (offsets % pool_side)[:, None]
    patch = jnp.arange(patch_rows, dtype=jnp.int32)[None, :]
    patch_i, patch_j = patch // GRID, patch % GRID
    kept = ((offsets >= 0) & (offsets < counts_kept))[:, None]
    inside = kept & (patch_i // 2 == token_i) & (patch_j // 2 == token_j) & (patch < GRID * GRID)
    high = jnp.minimum(2, GRID - 2 * token_i)
    wide = jnp.minimum(2, GRID - 2 * token_j)
    share = 1.0 / jnp.maximum(high * wide, 1).astype(jnp.float32)
    return jnp.where(inside, share, 0.0).astype(jnp.bfloat16)


def rotate(values, positions):
    head_dim = values.shape[-1]
    half_dim = head_dim // 2
    inv_rates = jnp.exp(
        jnp.arange(half_dim, dtype=jnp.float32) * (-2.0 * math.log(rope_base) / head_dim)
    )
    angles = positions.astype(jnp.float32)[:, None] * inv_rates[None, :]
    cosine = jnp.cos(angles)[:, None, :]
    sine_part = jnp.sin(angles)[:, None, :]
    first_half = values[..., :half_dim]
    second = values[..., half_dim:]
    return jnp.concatenate(
        [first_half * cosine - second * sine_part, second * cosine + first_half * sine_part],
        axis=-1,
    )


def per_device(
    patches,
    fc_gain,
    fc_in,
    fc_in_bias,
    fc_out,
    fc_out_bias,
    proj_weight,
    text_embed,
    frame_start,
    frame_count,
    segment_ids,
    norm_gain,
    query_weight,
    query_bias,
    key_weight,
    value_weight,
    value_bias,
):
    section_count = lax.axis_size("section")
    section_id = lax.axis_index("section")
    shard_id = lax.axis_index("seq")
    shard_rows = text_embed.shape[0]
    head_size = key_weight.shape[1]
    group_size = query_weight.shape[1] // head_size
    frame_patches = patches[0]
    patch_rows, feature_width = frame_patches.shape
    aligned = fc_in.shape[1] % 16 == 0 and lax.axis_size("seq") % 2 == 0
    if aligned:
        w_in, w_out_t = chain_gather((fc_in[0], fc_out[0].T), 0, pl.ANY)
        proj_weight, w_in, w_out_t = lax.optimization_barrier((proj_weight, w_in, w_out_t))
    else:
        w_in = lax.all_gather(fc_in, "seq", axis=1, tiled=True)[0]
        w_out = lax.all_gather(fc_out, "seq", axis=2, tiled=True)[0]
    proj_full = lax.all_gather(proj_weight, "seq", axis=0, tiled=True)
    layer_gain = fc_gain[0]
    bias_in = fc_in_bias[0]
    bias_out = fc_out_bias[0]
    batch_rows = 96 if aligned else 128
    batches = -(-patch_rows // batch_rows)
    padded_rows = batches * batch_rows
    frame_patches = jnp.pad(frame_patches, [(0, padded_rows - patch_rows), (0, 0)])
    first_section = section_id == 0
    last_section = section_id == section_count - 1
    if aligned:
        collected = encode(
            frame_patches, layer_gain, w_in, bias_in, w_out_t, bias_out, batch_rows, 1
        )
    else:
        results = []
        for tick in range(batches + 2 * (section_count - 1)):
            start = min(tick, batches - 1) * batch_rows
            block = frame_patches[start : start + batch_rows]
            if tick >= 2:
                inflow = passed_along(results[tick - 2], "section", 1)
                block = jnp.where(first_section, block, inflow)
            results.append(encoder_layer(block, layer_gain, w_in, bias_in, w_out, bias_out))
        collected = jnp.concatenate(results[2 * (section_count - 1) :], axis=0)
    local_slots = jnp.arange(shard_rows, dtype=jnp.int32)
    positions = shard_id * shard_rows + local_slots
    own_start = frame_start[shard_id]
    own_count = frame_count[shard_id]
    previous = jnp.maximum(shard_id - 1, 0)
    own_offsets = positions - own_start
    own_valid = (own_offsets >= 0) & (own_offsets < own_count)
    prev_offsets = positions - frame_start[previous]
    prev_valid = (shard_id > 0) & (prev_offsets >= 0) & (prev_offsets < frame_count[previous])
    wanted = jnp.concatenate([own_offsets, own_offsets + shard_rows])
    pooled = jnp.dot(
        pool_rows(wanted, own_count, padded_rows), collected, preferred_element_type=jnp.float32
    ).astype(jnp.bfloat16)
    arrived = passed_along(pooled[shard_rows:], "seq", 1)
    tokens = jnp.where(own_valid[:, None], pooled[:shard_rows], arrived)
    tokens = jnp.where(last_section, tokens, jnp.zeros_like(tokens))
    tokens = from_last(tokens, "section")
    vision = jnp.dot(tokens, proj_full, preferred_element_type=jnp.float32).astype(jnp.bfloat16)
    inputs = jnp.where((own_valid | prev_valid)[:, None], vision, text_embed)
    widened = inputs.astype(jnp.float32)
    normed = (
        widened
        * lax.rsqrt(jnp.mean(widened * widened, axis=1, keepdims=True) + rms_eps)
        * norm_gain
    ).astype(jnp.bfloat16)
    queries = jnp.dot(normed, query_weight, preferred_element_type=jnp.float32) + query_bias
    queries = rotate(queries.reshape(shard_rows, group_size, head_size), positions).astype(
        jnp.bfloat16
    )
    queries = queries.reshape(shard_rows * group_size, head_size)
    key_heads = jnp.dot(normed, key_weight, preferred_element_type=jnp.float32)
    key_heads = rotate(key_heads.reshape(shard_rows, 1, head_size), positions).astype(jnp.bfloat16)
    key_heads = key_heads.reshape(shard_rows, head_size)
    values = (
        jnp.dot(normed, value_weight, preferred_element_type=jnp.float32) + value_bias
    ).astype(jnp.bfloat16)
    stacked = jnp.concatenate([key_heads, values], axis=1)
    query_pos = jnp.repeat(positions, group_size)
    query_seg = jnp.repeat(
        lax.dynamic_slice_in_dim(segment_ids, shard_id * shard_rows, shard_rows, 0), group_size
    )
    if aligned:
        (arrived_rows,) = chain_gather((stacked,), 2, pltpu.VMEM)
    else:
        arrived_rows = lax.all_gather(stacked, "seq", axis=0, tiled=True)
    key_part = arrived_rows[:, :head_size]
    value_part = arrived_rows[:, head_size:]
    scores = lax.dot_general(
        queries, key_part, (((1,), (1,)), ((), ())), preferred_element_type=jnp.float32
    ) * (1.0 / math.sqrt(head_size))
    key_pos = jnp.arange(arrived_rows.shape[0], dtype=jnp.int32)
    allowed = (key_pos[None, :] <= query_pos[:, None]) & (
        segment_ids[None, :] == query_seg[:, None]
    )
    masked = jnp.where(allowed, scores, mask_floor)
    weights = jnp.where(allowed, jnp.exp(masked - jnp.max(masked, axis=1, keepdims=True)), 0.0)
    row_total = jnp.sum(weights, axis=1, keepdims=True)
    row_acc = jnp.dot(
        weights.astype(jnp.bfloat16), value_part, preferred_element_type=jnp.float32
    )
    attended = (row_acc / row_total).astype(jnp.bfloat16)
    return attended.reshape(shard_rows, group_size * head_size)


def solution(mesh):
    return jax.shard_map(
        per_device,
        mesh=mesh,
        in_specs=(
            P("seq", None, None),
            P("section", None),
            P("section", "seq", None),
            P("section", None),
            P("section", None, "seq"),
            P("section", None),
            P("seq", None),
            P("seq", None),
            P(),
            P(),
            P(),
            P(),
            P(None, "section"),
            P("section"),
            P(None, "section"),
            P(None, "section"),
            P("section"),
        ),
        out_specs=P("seq", "section"),
        check_vma=False,
    )
```

profile of v0, /device:TPU:29, one launch (start us, length us, event | category | flops | bytes accessed | tf_op | source)
XLA Modules:
  0.0 223.5 jit_solution(15135289627897302141)
XLA Ops:
  6.5 0.0 copy-start
  6.5 0.0 all-gather.2.cloned.1.call-start
  6.5 87.7 %shard_map.163 = (bf16[1152,2176]{1,0:T(8,128)(2,1)}, bf16[1152,2176]{1,0:T(8,128)(2,1)}) custom-call(bf16[144,2176]{1,0:T(8,128)(2,1)} %bitcast.26, bf16[144,2176]{1,0:T(8,128)(2,1)} %bitcast.27), custom_call_target="tpu_custom_call" | custom-call | tf_op jit(solution)/shard_map/pallas_call | solution.py:161
  94.2 0.0 copy-start.1
  94.2 0.0 copy-start.2
  94.3 0.0 copy-start.3
  94.3 0.0 all-gather.2.cloned.1.call-update
  94.3 0.0 copy-done.5
  94.3 0.1 pad.4.patches
  94.5 0.5 copy-done.1
  94.9 0.0 copy-done.2
  94.9 0.0 copy-done.3
  95.0 61.7 %shard_map.164 = bf16[768,1152]{1,0:T(8,128)(2,1)S(1)} custom-call(bf16[768,1152]{1,0:T(8,128)(2,1)S(1)} %pad.4.patches, f32[1,1152]{1,0:T(1,128)S(1)} %copy-done.2, bf16[1152,2176]{1,0:T(8,128)(2,1)} %get-tuple-element.12.w_in, f32[1,2176]{1,0:T(1,128)S(1)} %copy-done.1, bf16[1152,2176]{1,0:T(8,128)(2,1)} %get-tuple-element.13.w_out_t, f32[1,1152]{1,0:T(1,128)S(1)} %copy-done.3), custom_call_target="tpu_custom_call" | custom-call | tf_op jit(solution)/shard_map/pallas_call | solution.py:236
  156.7 0.0 copy-done.12
  156.7 0.0 copy-done.13
  156.7 0.6 fusion.57
  157.3 0.6 broadcast_add_fusion
  158.0 0.7 compare_and_fusion
  158.7 0.0 copy-start.10
  158.7 0.0 copy-start.7
  158.7 0.8 convolution_convert_fusion.1
  159.6 1.3 collective-permute-start
  160.9 0.0 copy-done.10
  160.9 0.1 dynamic_slice.15
  161.0 0.1 broadcast_in_dim.41
  161.1 0.1 eq.49
  161.2 0.1 broadcast_in_dim.40
  161.3 0.1 le.16
  161.4 1.8 and_or_fusion
  163.2 1.3 collective-permute-done
  164.5 0.1 fusion.17
  164.6 0.7 collective-permute-start.1
  165.3 0.7 collective-permute-start.2
  166.0 1.3 collective-permute-start.3
  167.3 0.3 multiply_cosine_fusion.1
  167.6 0.0 collective-permute-done.1
  167.6 0.0 collective-permute-done.2
  167.7 10.3 %collective-permute-done.3 = bf16[128,1152]{1,0:T(8,128)(2,1)S(1)} collective-permute-done((bf16[128,1152]{1,0:T(8,128)(2,1)S(1)}, bf16[128,1152]{1,0:T(8,128)(2,1)S(1)}, u32[]{:S(2)}, u32[]{:S(2)}) %collective-permute-start.3) | collective-permute-done | bytes 294944 | tf_op jit(solution)/shard_map/ppermute | solution.py:30
  177.9 0.0 copy-done.7
  177.9 5.0 %multiply_reduce_fusion = (f32[128]{0:T(128)S(1)}, f32[128,3584]{1,0:T(8,128)S(1)}) fusion(bf16[128,3584]{1,0:T(8,128)(2,1)S(1)} %copy-done.7, bf16[1152,3584]{1,0:T(8,128)(2,1)} %all-gather.2.cloned.1.call-done, bf16[128,1152]{1,0:T(8,128)(2,1)S(1)} %collective-permute-done.3, bf16[128,1152]{1,0:T(8,128)(2,1)S(1)} %collective-permute-done.2, ...), kind=kOutput, calls=%fused_computation.10 | convolution fusion | flops 1059700608 | bytes 12190336 | tf_op jit(solution)/shard_map/dot_general | solution.py:358
  182.9 0.0 copy-start.11
  182.9 0.0 copy-done.9
  182.9 0.2 multiply_convert_fusion
  183.2 0.0 copy-done.4
  183.2 0.4 copy-done.11
  183.6 0.6 convolution_add_fusion
  184.2 0.0 copy-start.6
  184.3 0.0 copy-start.14
  184.3 0.1 reshape.376
  184.4 0.0 copy-done
  184.4 0.4 convolution_bitcast_fusion
  184.8 0.3 fusion.36
  185.1 0.3 copy-done.6
  185.4 0.0 copy-done.14
  185.4 0.4 fusion.5
  185.8 0.7 pad_maximum_fusion.refs_0_
  186.5 25.6 %shard_map.165 = bf16[1024,256]{1,0:T(8,128)(2,1)} custom-call(bf16[128,256]{1,0:T(8,128)(2,1)} %pad_maximum_fusion.refs_0_), custom_call_target="tpu_custom_call" | custom-call | tf_op jit(solution)/shard_map/pallas_call | solution.py:161
  212.2 0.3 subtract_convert_fusion
  212.5 0.0 copy-start.8
  212.5 1.8 fusion.3
  214.3 0.9 fusion.6
  215.1 0.0 copy-done.8
  215.2 0.8 fusion.4
  216.0 0.7 reshape.378
  (13 shorter events, 0.1 us)
Async XLA Ops:
  6.5 177.8 %copy-start = (bf16[3584,128]{1,0:T(8,128)(2,1)S(1)}, bf16[3584,128]{1,0:T(8,128)(2,1)}, u32[]{:S(2)}) copy-start(bf16[3584,128]{1,0:T(8,128)(2,1)} %param.31) | copy-start | bytes 2752516
  6.5 87.8 %copy-start.5 = (bf16[1,729,1152]{2,1,0:T(8,128)(2,1)S(1)}, bf16[1,729,1152]{2,1,0:T(8,128)(2,1)}, u32[]{:S(2)}) copy-start(bf16[1,729,1152]{2,1,0:T(8,128)(2,1)} %param.17) | copy-start | bytes 5038852
  6.5 171.4 %all-gather.2.cloned.1.call-start = ((), (), s32[]{:S(2)}) async-start(), calls=%async_computation | async-start | bytes 9289728 | tf_op jit(solution)/shard_map/all_gather | solution.py:317
  94.2 0.7 copy-start.1
  94.2 0.7 copy-start.2
  94.3 0.7 copy-start.3
  95.0 61.7 %copy-start.12 = (s32[8]{0:T(128)S(1)}, s32[8]{0:T(128)}, u32[]{:S(2)}) copy-start(s32[8]{0:T(128)} %param.26) | copy-start | bytes 100
  95.0 61.7 %copy-start.13 = (s32[8]{0:T(128)S(1)}, s32[8]{0:T(128)}, u32[]{:S(2)}) copy-start(s32[8]{0:T(128)} %param.25) | copy-start | bytes 100
  158.7 2.2 copy-start.10
  158.7 19.2 %copy-start.7 = (bf16[128,3584]{1,0:T(8,128)(2,1)S(1)}, bf16[128,3584]{1,0:T(8,128)(2,1)}, u32[]{:S(2)}) copy-start(bf16[128,3584]{1,0:T(8,128)(2,1)} %param.24) | copy-start | bytes 2752516
  159.6 4.9 %collective-permute-start = (bf16[128,1152]{1,0:T(8,128)(2,1)S(1)}, bf16[128,1152]{1,0:T(8,128)(2,1)S(1)}, u32[]{:S(2)}, u32[]{:S(2)}) collective-permute-start(bf16[128,1152]{1,0:T(8,128)(2,1)S(1)} %slice.33), channel_id=1, source_target_pairs={{0,1},{1,2},{2,3},{3,4},{4,5},{5,6},{6,7},{8,9},{9,10},{10,11},{11... | collective-permute-start | bytes 884744 | tf_op jit(solution)/shard_map/ppermute | solution.py:23
  164.6 3.0 %collective-permute-start.1 = (bf16[128,1152]{1,0:T(8,128)(2,1)S(1)}, bf16[128,1152]{1,0:T(8,128)(2,1)S(1)}, u32[]{:S(2)}, u32[]{:S(2)}) collective-permute-start(bf16[128,1152]{1,0:T(8,128)(2,1)S(1)} %fusion.17), channel_id=1, source_target_pairs={{24,0},{25,1},{26,2},{27,3},{28,4},{29,5},{30,6},{31,7}} | collective-permute-start | bytes 884744 | tf_op jit(solution)/shard_map/ppermute | solution.py:30
  165.3 2.3 %collective-permute-start.2 = (bf16[128,1152]{1,0:T(8,128)(2,1)S(1)}, bf16[128,1152]{1,0:T(8,128)(2,1)S(1)}, u32[]{:S(2)}, u32[]{:S(2)}) collective-permute-start(bf16[128,1152]{1,0:T(8,128)(2,1)S(1)} %fusion.17), channel_id=1, source_target_pairs={{24,8},{25,9},{26,10},{27,11},{28,12},{29,13},{30,14},{31,15}} | collective-permute-start | bytes 884744 | tf_op jit(solution)/shard_map/ppermute | solution.py:30
  166.0 11.9 %collective-permute-start.3 = (bf16[128,1152]{1,0:T(8,128)(2,1)S(1)}, bf16[128,1152]{1,0:T(8,128)(2,1)S(1)}, u32[]{:S(2)}, u32[]{:S(2)}) collective-permute-start(bf16[128,1152]{1,0:T(8,128)(2,1)S(1)} %fusion.17), channel_id=1, source_target_pairs={{24,16},{25,17},{26,18},{27,19},{28,20},{29,21},{30,22},{31,23}} | collective-permute-start | bytes 884744 | tf_op jit(solution)/shard_map/ppermute | solution.py:30
  177.9 5.0 %copy-start.9 = (f32[3584]{0:T(1024)S(1)}, f32[3584]{0:T(1024)}, u32[]{:S(2)}) copy-start(f32[3584]{0:T(1024)} %param.28) | copy-start | bytes 43012
  177.9 5.3 %copy-start.4 = (bf16[3584,512]{1,0:T(8,128)(2,1)S(1)}, bf16[3584,512]{1,0:T(8,128)(2,1)}, u32[]{:S(2)}) copy-start(bf16[3584,512]{1,0:T(8,128)(2,1)} %param.29) | copy-start | bytes 11010052
  182.9 0.7 copy-start.11
  184.2 1.2 copy-start.6
  184.3 1.2 copy-start.14
  212.5 2.7 %copy-start.8 = (bf16[1024,256]{1,0:T(8,128)(2,1)S(1)}, bf16[1024,256]{1,0:T(8,128)(2,1)}, u32[]{:S(2)}) copy-start(bf16[1024,256]{1,0:T(8,128)(2,1)} %shard_map.165) | copy-start | bytes 1572868
Sparse Core Ops, SparseCore 0:
  94.4 81.8 all-gather.1
where the time goes:
time: 226 us; the launch traced here: 224 us
  Pallas kernels  175 us (77%)
  between operations  13.8 us (6%)
  waiting for transfers between devices  11.6 us (5%)
  matrix products  9.81 us (4%)
  other arithmetic  6.04 us (3%)
  starting transfers between devices  3.95 us (2%)
  local copies, waits for them, and re-layouts  3.38 us (1%)
    pallas_call x2, Pallas kernels, chain_gather(): pl.pallas_call(functools.partial(chain_kernel, count), out_shape=[jax.Sha...  113 us
    pallas_call x1, Pallas kernels, encode(): pl.pallas_call(functools.partial(encode_kernel, rows), out_shape=jax.Shap...  61.7 us
    ppermute x3, waiting for transfers between devices, from_last(): total = total + lax.ppermute(x, axis, [(last, other)])  10.3 us
    dot_general x1, matrix products, per_device(): jnp.dot(tokens, proj_full, preferred_element_type=jnp.float32)  4.97 us
  transfers between devices with their start and end apart: 5, of which 2 were waited for; matrix products, arithmetic and copies ran while one was open for 3% of the time, Pallas kernels for 28%

commit v1 on v0

--- a/solution.py
+++ b/solution.py
@@ -277,6 +277,252 @@
     return jnp.concatenate(
         [first_half * cosine - second * sine_part, second * cosine + first_half * sine_part],
         axis=-1,
+    )
+
+
+def tail_kernel(
+    tokens, text_h, proj_h, wq_h, wk_h, wv_h, gain, q_bias, v_bias, turn, segs, starts, counts,
+    out, text, proj, wq, wk, wv, held, queries, pairs, load_s, send_s, recv_s, pass_s, got_s,
+):
+    size = lax.axis_size("seq")
+    chips = size // 2
+    me = lax.axis_index("seq")
+    chip, core = me // 2, me % 2
+    partner = chip * 2 + 1 - core
+    rows, hm = text_h.shape
+    head = wk_h.shape[1]
+    group = wq_h.shape[1] // head
+    tile = math.gcd(hm, 512)
+    tiles = hm // tile
+
+    def part(t):
+        return pltpu.make_async_copy(
+            proj_h.at[:, pl.ds(t * tile, tile)], proj.at[:, pl.ds(t * tile, tile)], load_s.at[t]
+        )
+
+    others = [(text_h, text), (wq_h, wq), (wk_h, wk), (wv_h, wv)]
+    loads = [
+        pltpu.make_async_copy(a, b, load_s.at[tiles + i]) for i, (a, b) in enumerate(others)
+    ]
+    loads[0].start()
+    for t in range(tiles):
+        part(t).start()
+    for load in loads[1:]:
+        load.start()
+
+    barrier = pltpu.get_barrier_semaphore()
+
+    def hail(other, carry):
+        @pl.when(other != chip)
+        def _():
+            pl.semaphore_signal(
+                barrier, inc=1, device_id={"seq": other * 2 + core}, device_id_type=MESH
+            )
+
+        return carry
+
+    lax.fori_loop(0, chips, hail, 0)
+    pl.semaphore_signal(barrier, inc=1, device_id={"seq": partner}, device_id_type=MESH)
+
+    slot = lax.broadcasted_iota(jnp.int32, (rows, 1), 0) + me * rows
+    before = jnp.maximum(me - 1, 0)
+    own = slot - starts[me]
+    prev = slot - starts[before]
+    valid = ((own >= 0) & (own < counts[me])) | (
+        (me > 0) & (prev >= 0) & (prev < counts[before])
+    )
+    loads[0].wait()
+    squares = jnp.zeros((rows, 1), jnp.float32)
+    for t in range(tiles):
+        cols = slice(t * tile, (t + 1) * tile)
+        part(t).wait()
+        vision = jnp.dot(tokens[...], proj[:, cols], preferred_element_type=jnp.float32)
+        mixed = jnp.where(
+            valid, vision.astype(jnp.bfloat16).astype(jnp.float32), text[:, cols].astype(jnp.float32)
+        )
+        squares = squares + jnp.sum(mixed * mixed, axis=1, keepdims=True)
+        held[:, cols] = mixed.astype(jnp.bfloat16)
+    scale = lax.rsqrt(squares / hm + rms_eps)
+    for t in range(tiles):
+        cols = slice(t * tile, (t + 1) * tile)
+        held[:, cols] = (held[:, cols].astype(jnp.float32) * scale * gain[:, cols]).astype(
+            jnp.bfloat16
+        )
+    for load in loads[1:]:
+        load.wait()
+    half = head // 2
+    cosine, sine = turn[:, :head], turn[:, head:]
+
+    def spun(u):
+        return u * cosine + jnp.concatenate([u[:, half:], u[:, :half]], axis=1) * sine
+
+    normed = held[...]
+    mine = pl.ds(pl.multiple_of(me * rows, rows), rows)
+    keys = jnp.dot(normed, wk[...], preferred_element_type=jnp.float32)
+    pairs[mine, :head] = spun(keys).astype(jnp.bfloat16)
+    values = jnp.dot(normed, wv[...], preferred_element_type=jnp.float32) + v_bias[...]
+    pairs[mine, head:] = values.astype(jnp.bfloat16)
+
+    pl.semaphore_wait(barrier, chips)
+
+    def above(other):
+        return pltpu.make_async_remote_copy(
+            src_ref=pairs.at[mine],
+            dst_ref=pairs.at[mine],
+            send_sem=send_s.at[other],
+            recv_sem=recv_s.at[chip],
+            device_id={"seq": other * 2 + core},
+            device_id_type=MESH,
+        )
+
+    def across(source):
+        block = pl.ds(pl.multiple_of((source * 2 + core) * rows, rows), rows)
+        return pltpu.make_async_remote_copy(
+            src_ref=pairs.at[block],
+            dst_ref=pairs.at[block],
+            send_sem=pass_s.at[source],
+            recv_sem=got_s.at[source],
+            device_id={"seq": partner},
+            device_id_type=MESH,
+        )
+
+    def arriving(source, core_of, send, recv, target):
+        block = pl.ds(pl.multiple_of((source * 2 + core_of) * rows, rows), rows)
+        return pltpu.make_async_remote_copy(
+            src_ref=pairs.at[block],
+            dst_ref=pairs.at[block],
+            send_sem=send.at[source],
+            recv_sem=recv.at[source],
+            device_id={"seq": target},
+            device_id_type=MESH,
+        )
+
+    across(chip).start()
+
+    def push(other, carry):
+        above(other).start()
+        return carry
+
+    lax.fori_loop(chip + 1, chips, push, 0)
+    asked = jnp.dot(normed, wq[...], preferred_element_type=jnp.float32) + q_bias[...]
+    for h in range(group):
+        queries[h * rows : (h + 1) * rows, :] = spun(asked[:, h * head : (h + 1) * head]).astype(
+            jnp.bfloat16
+        )
+
+    def relay(i, carry):
+        source = chip - 1 - i
+        arriving(source, core, send_s, recv_s, partner).wait_recv()
+        across(source).start()
+        return carry
+
+    lax.fori_loop(0, chip, relay, 0)
+
+    def widened(j):
+        row = segs[pl.ds(j, 1), :].astype(jnp.float32)
+        return jnp.broadcast_to(row, (rows, rows))
+
+    seg_q = widened(me).T
+    seg_q = jnp.concatenate([seg_q, seg_q], axis=1)
+    row_i = lax.broadcasted_iota(jnp.int32, (rows, 2 * rows), 0) + me * rows
+    col_i = lax.broadcasted_iota(jnp.int32, (rows, 2 * rows), 1)
+    spread = 1.0 / math.sqrt(head)
+
+    def attend(i, carry):
+        top, total, acc = carry
+        source = chip - i
+        arriving(source, 1 - core, pass_s, got_s, partner).wait_recv()
+        block = pl.ds(pl.multiple_of(source * 2 * rows, 2 * rows), 2 * rows)
+        seg_k = jnp.concatenate([widened(source * 2), widened(source * 2 + 1)], axis=1)
+        allowed = (col_i + source * 2 * rows <= row_i) & (seg_k == seg_q)
+        allowed = jnp.concatenate([jnp.where(allowed, 1.0, 0.0)] * group, axis=0) > 0.5
+        score = (
+            lax.dot_general(
+                queries[...],
+                pairs[block, :head],
+                (((1,), (1,)), ((), ())),
+                preferred_element_type=jnp.float32,
+            )
+            * spread
+        )
+        score = jnp.where(allowed, score, mask_floor)
+        best = jnp.maximum(top, jnp.max(score, axis=1, keepdims=True))
+        weight = jnp.where(allowed, jnp.exp(score - best), 0.0)
+        fade = jnp.exp(top - best)
+        total = total * fade + jnp.sum(weight, axis=1, keepdims=True)
+        acc = acc * fade + jnp.dot(
+            weight.astype(jnp.bfloat16), pairs[block, head:], preferred_element_type=jnp.float32
+        )
+        return best, total, acc
+
+    start = (
+        jnp.full((group * rows, 1), mask_floor, jnp.float32),
+        jnp.zeros((group * rows, 1), jnp.float32),
+        jnp.zeros((group * rows, head), jnp.float32),
+    )
+    _, total, acc = lax.fori_loop(0, chip + 1, attend, start)
+    result = (acc / total).astype(jnp.bfloat16)
+    for h in range(group):
+        out[:, h * head : (h + 1) * head] = result[h * rows : (h + 1) * rows, :]
+
+    def drain_push(other, carry):
+        above(other).wait_send()
+        return carry
+
+    lax.fori_loop(chip + 1, chips, drain_push, 0)
+
+    def drain_pass(source, carry):
+        across(source).wait_send()
+        return carry
+
+    lax.fori_loop(0, chip + 1, drain_pass, 0)
+
+
+def tail(tokens, text, proj, wq, wk, wv, gain, q_bias, v_bias, segment_ids, starts, counts, call_id):
+    size = lax.axis_size("seq")
+    chips = size // 2
+    rows, hm = text.shape
+    head = wk.shape[1]
+    group = wq.shape[1] // head
+    half = head // 2
+    positions = lax.axis_index("seq") * rows + jnp.arange(rows, dtype=jnp.int32)
+    rates = jnp.exp(
+        jnp.arange(half, dtype=jnp.float32) * (-2.0 * math.log(rope_base) / head)
+    )
+    angles = positions.astype(jnp.float32)[:, None] * rates[None, :]
+    c, s = jnp.cos(angles), jnp.sin(angles)
+    turn = jnp.concatenate([c, c, -s, s], axis=1)
+    tiles = hm // math.gcd(hm, 512)
+    whole = pl.BlockSpec(memory_space=pltpu.VMEM)
+    far = pl.BlockSpec(memory_space=pl.ANY)
+    small = pl.BlockSpec(memory_space=pltpu.SMEM)
+    dma = pltpu.SemaphoreType.DMA
+    return pl.pallas_call(
+        tail_kernel,
+        out_shape=jax.ShapeDtypeStruct((rows, group * head), jnp.bfloat16),
+        in_specs=[whole] + [far] * 5 + [whole] * 5 + [small] * 2,
+        out_specs=whole,
+        scratch_shapes=[
+            pltpu.VMEM(text.shape, text.dtype),
+            pltpu.VMEM(proj.shape, proj.dtype),
+            pltpu.VMEM(wq.shape, wq.dtype),
+            pltpu.VMEM(wk.shape, wk.dtype),
+            pltpu.VMEM(wv.shape, wv.dtype),
+            pltpu.VMEM((rows, hm), jnp.bfloat16),
+            pltpu.VMEM((group * rows, head), jnp.bfloat16),
+            pltpu.VMEM((size * rows, 2 * head), jnp.bfloat16),
+            dma((tiles + 4,)),
+            dma((chips,)),
+            dma((chips,)),
+            dma((chips,)),
+            dma((chips,)),
+        ],
+        compiler_params=pltpu.CompilerParams(
+            collective_id=call_id, has_side_effects=True, vmem_limit_bytes=48 * 1024 * 1024
+        ),
+    )(
+        tokens, text, proj, wq, wk, wv, gain[None], q_bias[None], v_bias[None], turn,
+        segment_ids.reshape(size, rows), starts, counts,
     )
 
 
@@ -355,6 +601,11 @@
     tokens = jnp.where(own_valid[:, None], pooled[:shard_rows], arrived)
     tokens = jnp.where(last_section, tokens, jnp.zeros_like(tokens))
     tokens = from_last(tokens, "section")
+    if aligned:
+        return tail(
+            tokens, text_embed, proj_full, query_weight, key_weight, value_weight, norm_gain,
+            query_bias, value_bias, segment_ids, frame_start, frame_count, 2,
+        )
     vision = jnp.dot(tokens, proj_full, preferred_element_type=jnp.float32).astype(jnp.bfloat16)
     inputs = jnp.where((own_valid | prev_valid)[:, None], vision, text_embed)
     widened = inputs.astype(jnp.float32)

time: 226 us -> 214 us (0.947)
  the two profiles are of different devices: /device:TPU:29 before, /device:TPU:25 now
where the time goes in v1:
time: 214 us
  Pallas kernels  157 us (73%)
  waiting for transfers between devices  31.1 us (15%)
  between operations  13.7 us (6%)
  starting transfers between devices  4.06 us (2%)
  other arithmetic  3.64 us (2%)
  local copies, waits for them, and re-layouts  2.85 us (1%)
    pallas_call x1, Pallas kernels, chain_gather(): pl.pallas_call(functools.partial(chain_kernel, count), out_shape=[jax.Sha...  87.7 us
    pallas_call x1, Pallas kernels, encode(): pl.pallas_call(functools.partial(encode_kernel, rows), out_shape=jax.Shap...  45.7 us
    ppermute x3, waiting for transfers between devices, from_last(): total = total + lax.ppermute(x, axis, [(last, other)])  27.9 us
    pallas_call x1, Pallas kernels, tail(): pl.pallas_call(tail_kernel, out_shape=jax.ShapeDtypeStruct((rows, group *...  24 us
  transfers between devices with their start and end apart: 5, of which 2 were waited for; matrix products, arithmetic and copies ran while one was open for 3% of the time, Pallas kernels for 21%

profile of v1, /device:TPU:25, one launch (start us, length us, event | category | flops | bytes accessed | tf_op | source)
XLA Modules:
  0.0 213.6 jit_solution(783917060981836799)
XLA Ops:
  6.5 0.0 copy-start.8
  6.5 0.0 copy-start.9
  6.5 0.0 copy-start.11
  6.5 0.0 all-gather.2.cloned.1.call-start
  6.5 87.7 %shard_map.163 = (bf16[1152,2176]{1,0:T(8,128)(2,1)}, bf16[1152,2176]{1,0:T(8,128)(2,1)}) custom-call(bf16[144,2176]{1,0:T(8,128)(2,1)} %bitcast.15, bf16[144,2176]{1,0:T(8,128)(2,1)} %bitcast.16), custom_call_target="tpu_custom_call" | custom-call | tf_op jit(solution)/shard_map/pallas_call | solution.py:161
  94.2 0.0 all-gather.2.cloned.1.call-update
  94.2 0.0 copy-start.3
  94.3 0.0 copy-start.4
  94.3 0.0 copy-start.5
  94.3 0.0 copy-done.8
  94.3 0.6 dynamic_slice.7
  94.9 0.0 copy-done.9
  94.9 0.6 dynamic_slice.6
  95.5 0.0 copy-done.11
  95.5 0.1 pad.4.patches
  95.7 0.0 copy-done.3
  95.7 0.0 copy-done.4
  95.7 0.0 copy-done.5
  95.7 45.7 %shard_map.164 = bf16[768,1152]{1,0:T(8,128)(2,1)S(1)} custom-call(bf16[768,1152]{1,0:T(8,128)(2,1)S(1)} %pad.4.patches, f32[1,1152]{1,0:T(1,128)S(1)} %copy-done.4, bf16[1152,2176]{1,0:T(8,128)(2,1)} %get-tuple-element.12.w_in, f32[1,2176]{1,0:T(1,128)S(1)} %copy-done.3, bf16[1152,2176]{1,0:T(8,128)(2,1)} %get-tuple-element.13.w_out_t, f32[1,1152]{1,0:T(1,128)S(1)} %copy-done.5), custom_call_target="tpu_custom_call" | custom-call | tf_op jit(solution)/shard_map/pallas_call | solution.py:236
  141.4 1.3 compare_and_fusion.1
  142.8 0.7 compare_and_fusion
  143.5 0.0 copy-start.12
  143.5 0.9 convolution_convert_fusion
  144.4 0.0 copy-start
  144.4 0.0 copy-start.1
  144.4 0.0 copy-start.2
  144.4 0.0 copy-start.6
  144.4 0.0 copy-start.7
  144.4 0.0 copy-start.10
  144.4 0.7 slice.9
  145.2 1.4 collective-permute-start
  146.6 0.0 copy-done.12
  146.7 3.1 %collective-permute-done = bf16[128,1152]{1,0:T(8,128)(2,1)} collective-permute-done((bf16[128,1152]{1,0:T(8,128)(2,1)}, bf16[128,1152]{1,0:T(8,128)(2,1)}, u32[]{:S(2)}, u32[]{:S(2)}) %collective-permute-start) | collective-permute-done | bytes 294944 | tf_op jit(solution)/shard_map/ppermute | solution.py:23
  149.8 1.1 fusion.8
  150.9 0.7 collective-permute-start.3
  151.6 0.7 collective-permute-start.2
  152.3 1.3 collective-permute-start.1
  153.6 0.3 multiply_cosine_fusion
  153.9 0.1 pad_maximum_fusion.turn
  154.0 0.0 collective-permute-done.3
  154.0 0.0 collective-permute-done.2
  154.0 27.9 %collective-permute-done.1 = bf16[128,1152]{1,0:T(8,128)(2,1)S(1)} collective-permute-done((bf16[128,1152]{1,0:T(8,128)(2,1)S(1)}, bf16[128,1152]{1,0:T(8,128)(2,1)S(1)}, u32[]{:S(2)}, u32[]{:S(2)}) %collective-permute-start.1) | collective-permute-done | bytes 294944 | tf_op jit(solution)/shard_map/ppermute | solution.py:30
  182.0 0.1 add_add_fusion.tokens
  182.0 0.0 all-gather.2.cloned.1.call-done.proj_h
  182.1 0.0 copy-done
  182.1 0.0 copy-done.1
  182.1 0.0 copy-done.2
  182.1 0.0 copy-done.6
  182.1 0.0 copy-done.7
  182.1 0.0 copy-done.10
  182.1 24.0 %shard_map.165 = bf16[128,512]{1,0:T(8,128)(2,1)S(1)} custom-call(bf16[128,1152]{1,0:T(8,128)(2,1)S(1)} %add_add_fusion.tokens, bf16[128,3584]{1,0:T(8,128)(2,1)S(1)} %copy-done, bf16[1152,3584]{1,0:T(8,128)(2,1)} %all-gather.2.cloned.1.call-done.proj_h, bf16[3584,512]{1,0:T(8,128)(2,1)} %wq_h.1, bf16[3584,128]{1,0:T(8,128)(2,1)S(1)} %copy-done.1, ...), custom_call_target="tpu_custom_call" | custom-call | tf_op jit(solution)/shard_map/pallas_call | solution.py:500
  206.1 0.7 copy.20
  (7 shorter events, 0.1 us)
Async XLA Ops:
  6.5 87.8 %copy-start.8 = (s32[8]{0:T(128)S(1)}, s32[8]{0:T(128)}, u32[]{:S(2)}) copy-start(s32[8]{0:T(128)} %counts.1) | copy-start | bytes 100
  6.5 88.4 %copy-start.9 = (s32[8]{0:T(128)S(1)}, s32[8]{0:T(128)}, u32[]{:S(2)}) copy-start(s32[8]{0:T(128)} %starts.1) | copy-start | bytes 100
  6.5 89.0 %copy-start.11 = (bf16[1,729,1152]{2,1,0:T(8,128)(2,1)S(1)}, bf16[1,729,1152]{2,1,0:T(8,128)(2,1)}, u32[]{:S(2)}) copy-start(bf16[1,729,1152]{2,1,0:T(8,128)(2,1)} %param.17) | copy-start | bytes 5038852
  6.5 175.5 %all-gather.2.cloned.1.call-start = ((), (), s32[]{:S(2)}) async-start(), calls=%async_computation | async-start | bytes 9289728 | tf_op jit(solution)/shard_map/all_gather | solution.py:563
  94.2 1.4 copy-start.3
  94.3 1.4 copy-start.4
  94.3 1.4 copy-start.5
  143.5 3.1 %copy-start.12 = (f32[3584]{0:T(1024)S(1)}, f32[3584]{0:T(1024)}, u32[]{:S(2)}) copy-start(f32[3584]{0:T(1024)} %param.28) | copy-start | bytes 43012
  144.4 37.7 %copy-start = (bf16[128,3584]{1,0:T(8,128)(2,1)S(1)}, bf16[128,3584]{1,0:T(8,128)(2,1)}, u32[]{:S(2)}) copy-start(bf16[128,3584]{1,0:T(8,128)(2,1)} %text_h.1) | copy-start | bytes 2752516
  144.4 37.7 %copy-start.1 = (bf16[3584,128]{1,0:T(8,128)(2,1)S(1)}, bf16[3584,128]{1,0:T(8,128)(2,1)}, u32[]{:S(2)}) copy-start(bf16[3584,128]{1,0:T(8,128)(2,1)} %wk_h.1) | copy-start | bytes 2752516
  144.4 37.7 %copy-start.2 = (bf16[3584,128]{1,0:T(8,128)(2,1)S(1)}, bf16[3584,128]{1,0:T(8,128)(2,1)}, u32[]{:S(2)}) copy-start(bf16[3584,128]{1,0:T(8,128)(2,1)} %wv_h.1) | copy-start | bytes 2752516
  144.4 37.7 %copy-start.6 = (s32[1024]{0:T(1024)S(1)}, s32[1024]{0:T(1024)}, u32[]{:S(2)}) copy-start(s32[1024]{0:T(1024)} %param.27) | copy-start | bytes 12292
  144.4 37.7 %copy-start.7 = (f32[512]{0:T(512)S(1)}, f32[512]{0:T(512)}, u32[]{:S(2)}) copy-start(f32[512]{0:T(512)} %param.30) | copy-start | bytes 6148
  144.4 37.7 %copy-start.10 = (f32[128]{0:T(128)S(1)}, f32[128]{0:T(128)}, u32[]{:S(2)}) copy-start(f32[128]{0:T(128)} %param.33) | copy-start | bytes 1540
  145.2 4.6 %collective-permute-start = (bf16[128,1152]{1,0:T(8,128)(2,1)}, bf16[128,1152]{1,0:T(8,128)(2,1)}, u32[]{:S(2)}, u32[]{:S(2)}) collective-permute-start(bf16[128,1152]{1,0:T(8,128)(2,1)} %slice.9), channel_id=1, source_target_pairs={{0,1},{1,2},{2,3},{3,4},{4,5},{5,6},{6,7},{8,9},{9,10},{10,11},{11... | collective-permute-start | bytes 884744 | tf_op jit(solution)/shard_map/ppermute | solution.py:23
  150.9 3.1 %collective-permute-start.3 = (bf16[128,1152]{1,0:T(8,128)(2,1)S(1)}, bf16[128,1152]{1,0:T(8,128)(2,1)S(1)}, u32[]{:S(2)}, u32[]{:S(2)}) collective-permute-start(bf16[128,1152]{1,0:T(8,128)(2,1)S(1)} %fusion.8), channel_id=1, source_target_pairs={{24,16},{25,17},{26,18},{27,19},{28,20},{29,21},{30,22},{31,23}} | collective-permute-start | bytes 884744 | tf_op jit(solution)/shard_map/ppermute | solution.py:30
  151.6 2.4 %collective-permute-start.2 = (bf16[128,1152]{1,0:T(8,128)(2,1)S(1)}, bf16[128,1152]{1,0:T(8,128)(2,1)S(1)}, u32[]{:S(2)}, u32[]{:S(2)}) collective-permute-start(bf16[128,1152]{1,0:T(8,128)(2,1)S(1)} %fusion.8), channel_id=1, source_target_pairs={{24,8},{25,9},{26,10},{27,11},{28,12},{29,13},{30,14},{31,15}} | collective-permute-start | bytes 884744 | tf_op jit(solution)/shard_map/ppermute | solution.py:30
  152.3 29.7 %collective-permute-start.1 = (bf16[128,1152]{1,0:T(8,128)(2,1)S(1)}, bf16[128,1152]{1,0:T(8,128)(2,1)S(1)}, u32[]{:S(2)}, u32[]{:S(2)}) collective-permute-start(bf16[128,1152]{1,0:T(8,128)(2,1)S(1)} %fusion.8), channel_id=1, source_target_pairs={{24,0},{25,1},{26,2},{27,3},{28,4},{29,5},{30,6},{31,7}} | collective-permute-start | bytes 884744 | tf_op jit(solution)/shard_map/ppermute | solution.py:30
Sparse Core Ops, SparseCore 0:
  94.4 82.0 all-gather.1
